TPU v7x, 512 devices: a whole 4x4x16 slice. The times are simulated.
512 devices in a mesh: seq: 64 (over x, z), head: 8 (over y, core).
Axes of the slice: x: 4, y: 4, z: 16, core: 2. Of those that a mesh axis runs over, the one named last changes fastest.
Arguments:
- queries: bfloat16 [16384, 4096], P('seq', 'head'), may hold values from -12 to 12
- key_input: bfloat16 [16384, 4096], P('seq', 'head'), may hold values from -1.796875 to 1.796875
- value_input: bfloat16 [16384, 4096], P('seq', 'head'), may hold values from -32 to 32
- norm_gain: bfloat16 [4096], P('head'), may hold values from 0.099609375 to 1.8984375
- out_weight: bfloat16 [4096, 3072], P('head', 'seq'), may hold values from -0.25 to 0.25
- target: bfloat16 [16384, 3072], P('seq', 'head'), may hold values from -6 to 6
Outputs:
- output: bfloat16 [16384, 3072], P('seq', 'head')
- query_grad: bfloat16 [16384, 4096], P('seq', 'head')
- key_grad: bfloat16 [16384, 4096], P('seq', 'head')
- value_grad: bfloat16 [16384, 4096], P('seq', 'head')
- gain_grads: float32 [64, 4096], P('seq', 'head')
- weight_grads: bfloat16 [64, 4096, 3072], P('seq', 'head')
All inputs are finite; a program needn't handle non-finite values.
Results may differ from a plain program's by a relative error of at most 0.022.
Values may be sent and summed in bfloat16 or wider, within the bound.
No kernel may reach another device: no remote copies, remote signals or barrier semaphores. Data moves between devices by JAX's collectives and lax.ppermute only.
A program may use at most 64 MiB of HBM per device.

v0:
```python
import jax
import jax.numpy as jnp
from jax import lax
from jax.sharding import Mesh
from jax.sharding import PartitionSpec as P

HEAD_DIM = 128
FEATURES = 4096
SEQ = ("seq_0", "seq_1")
EPSILON = 1e-06


def filled_with(shard, identity):
    return jnp.zeros_like(shard) + jnp.asarray(identity, shard.dtype)


def carried_in(shard, axes, combine, identity, reverse):
    before = start = filled_with(shard, identity)
    total = shard
    for axis in reversed(axes):
        length, index = (lax.axis_size(axis), lax.axis_index(axis))
        pieces = lax.all_gather(total.astype(jnp.bfloat16), axis)
        inside, total = (start, start)
        for k in reversed(range(length)) if reverse else range(length):
            passed = k > index if reverse else k < index
            total = combine(total, pieces[k].astype(shard.dtype))
            inside = jnp.where(passed, total, inside)
        before = combine(inside, before)
    return before


def laid_out(pieces, dim):
    pieces = jnp.moveaxis(pieces, 0, dim)
    dims = pieces.shape
    return pieces.reshape(*dims[:dim], dims[dim] * dims[dim + 1], *dims[dim + 2 :])


def gather_in_order(shard, axes, turns):
    pieces = shard[None]
    for k in turns:
        pieces = lax.all_gather(pieces, axes[k], axis=0, tiled=True)
    held = [lax.axis_size(axes[k]) for k in reversed(turns)]
    pieces = pieces.reshape(*held, *shard.shape)
    turned = sorted(range(len(turns)), key=lambda place: turns[len(turns) - 1 - place])
    return pieces.transpose(*turned, *range(len(turns), pieces.ndim)).reshape(-1, *shard.shape)


def gathered_by_axis(shard, axes, turns, dim):
    return laid_out(gather_in_order(shard, axes, turns), dim)


def in_blocks(shard, dim, length):
    before, after = (shard.shape[:dim], shard.shape[dim + 1 :])
    return jnp.moveaxis(shard.reshape(*before, length, -1, *after), dim, 0)


def summed_on_arrival(shard, axis, dim):
    length = lax.axis_size(axis)
    pieces = lax.all_to_all(in_blocks(shard, dim, length), axis, 0, 0, tiled=True)
    return jnp.sum(pieces.astype(jnp.float32), axis=0)


def causal(count):
    row_index = lax.broadcasted_iota(jnp.int32, (count, count), 0)
    col_index = lax.broadcasted_iota(jnp.int32, (count, count), 1)
    return row_index >= col_index


def add_states(earlier, later):
    return earlier + later


def per_device(queries, key_input, value_input, norm_gain, out_weight, target):
    tok_count = queries.shape[0]
    local_heads = queries.shape[1] // HEAD_DIM
    shape3 = (tok_count, local_heads, HEAD_DIM)
    q_heads = queries.reshape(shape3)
    k_heads = key_input.reshape(shape3)
    v_heads = value_input.reshape(shape3)
    keep_mask = causal(tok_count)
    f32 = jnp.float32
    state_local = jnp.einsum("shd,she->hde", k_heads, v_heads, preferred_element_type=f32)
    zero_state = jnp.zeros_like(state_local)
    earlier_state = carried_in(state_local, SEQ, add_states, zero_state, False)
    state_low = earlier_state.astype(jnp.bfloat16)
    scores = jnp.einsum("thd,shd->hts", q_heads, k_heads, preferred_element_type=f32)
    scores_low = jnp.where(keep_mask[None], scores, 0.0).astype(jnp.bfloat16)
    attended = jnp.einsum("hts,shd->thd", scores_low, v_heads, preferred_element_type=f32)
    attended = attended + jnp.einsum("thd,hde->the", q_heads, state_low, preferred_element_type=f32)
    mixed = attended.reshape(tok_count, -1)
    gain_float = norm_gain.astype(f32)
    squares = lax.psum(jnp.sum(mixed * mixed, axis=1, keepdims=True), "head")
    inverse = lax.rsqrt(squares / FEATURES + EPSILON)
    normed = (mixed * inverse * gain_float).astype(jnp.bfloat16)
    full_weight = gathered_by_axis(out_weight, SEQ, (0, 1), 1)
    partial_value = jnp.dot(normed, full_weight, preferred_element_type=f32)
    projected = summed_on_arrival(partial_value.astype(jnp.bfloat16), "head", 1)
    output = projected.astype(jnp.bfloat16)
    grad_local = (projected - target.astype(f32)).astype(jnp.bfloat16)
    out_grad = lax.all_gather(grad_local, "head", axis=1, tiled=True)
    normed_grad = lax.dot_general(
        out_grad, full_weight, (((1,), (1,)), ((), ())), preferred_element_type=f32
    )
    product = jnp.sum(grad_local.astype(f32) * projected, axis=1, keepdims=True)
    inner = lax.psum(product, "head") / inverse
    mixed_grad = inverse * gain_float * normed_grad - mixed * inverse**3 * inner / FEATURES
    mixed_grad = mixed_grad.astype(jnp.bfloat16)
    gain_grads = jnp.sum(normed_grad * mixed * inverse, axis=0)[None]
    weight_grads = lax.dot_general(
        normed, out_grad, (((0,), (0,)), ((), ())), preferred_element_type=f32
    ).astype(jnp.bfloat16)[None]
    grad_heads = mixed_grad.reshape(shape3)
    grad_state = jnp.einsum("thd,the->hde", q_heads, grad_heads, preferred_element_type=f32)
    later_state = carried_in(grad_state, SEQ, add_states, zero_state, True)
    later_low = later_state.astype(jnp.bfloat16)
    pairs = jnp.einsum("thd,shd->hts", grad_heads, v_heads, preferred_element_type=f32)
    pairs_low = jnp.where(keep_mask[None], pairs, 0.0).astype(jnp.bfloat16)
    query_grad = jnp.einsum("hts,shd->thd", pairs_low, k_heads, preferred_element_type=f32)
    query_grad = query_grad + jnp.einsum(
        "the,hde->thd", grad_heads, state_low, preferred_element_type=f32
    )
    key_grad = jnp.einsum("hts,thd->shd", pairs_low, q_heads, preferred_element_type=f32)
    key_grad = key_grad + jnp.einsum("she,hde->shd", v_heads, later_low, preferred_element_type=f32)
    value_grad = jnp.einsum("hts,the->she", scores_low, grad_heads, preferred_element_type=f32)
    value_grad = value_grad + jnp.einsum(
        "shd,hde->she", k_heads, later_low, preferred_element_type=f32
    )
    flat_shape = (tok_count, -1)
    return (
        output,
        query_grad.reshape(flat_shape).astype(jnp.bfloat16),
        key_grad.reshape(flat_shape).astype(jnp.bfloat16),
        value_grad.reshape(flat_shape).astype(jnp.bfloat16),
        gain_grads,
        weight_grads,
    )


def solution(mesh):
    torus = Mesh(mesh.devices.reshape(4, 16, mesh.shape["head"]), ("seq_0", "seq_1", "head"))
    return jax.shard_map(
        per_device,
        mesh=torus,
        in_specs=(
            P(SEQ, "head"),
            P(SEQ, "head"),
            P(SEQ, "head"),
            P("head"),
            P("head", SEQ),
            P(SEQ, "head"),
        ),
        out_specs=(
            P(SEQ, "head"),
            P(SEQ, "head"),
            P(SEQ, "head"),
            P(SEQ, "head"),
            P(SEQ, "head"),
            P(SEQ, "head", None),
        ),
        check_vma=False,
    )
```

profile of v0, /device:TPU:8, one launch (start us, length us, event | category | flops | bytes accessed | tf_op | source)
XLA Modules:
  0.0 324.0 jit_solution(6673106634308341939)
XLA Ops:
  7.3 1.1 copy.193
  8.4 1.9 convolution_convert_fusion.3
  10.4 0.0 all-gather.8.cloned.1.call-start
  10.4 12.7 %all-gather.1 = bf16[2048,48]{0,1:T(8,128)(2,1)S(1)} all-gather(bf16[512,48]{0,1:T(8,128)(2,1)} %param.10), channel_id=3, replica_groups=mesh['seq_0'=4,'seq_1'=16,'head'=8] {'seq_0'}, dimensions={0}, use_global_device_ids=true | all-gather | bytes 245760 | tf_op jit(solution)/shard_map/all_gather | solution.py:41
  23.1 0.7 copy.197
  23.8 0.0 all-gather.10.cloned.1.call-start
  24.0 0.3 fusion.1
  24.3 0.3 copy-done.15
  24.6 0.8 copy-done.9
  25.4 0.3 convolution_bitcast_fusion.5
  25.7 62.0 %all-gather.12.cloned.1.call-done = bf16[64,128,128]{2,1,0:T(8,128)(2,1)} async-done(((bf16[4,128,128]{2,1,0:T(8,128)(2,1)}), bf16[64,128,128]{2,1,0:T(8,128)(2,1)}) %all-gather.12.cloned.1.call-update) | async-done | bytes 2097168 | tf_op jit(solution)/shard_map/all_gather | solution.py:22
  87.7 2.1 fusion.46
  89.8 13.1 %all_gather.31 = bf16[4,4,128,128]{3,2,1,0:T(8,128)(2,1)S(1)} all-gather(bf16[1,4,128,128]{3,2,1,0:T(8,128)(2,1)S(1)} %fusion.46), channel_id=1, replica_groups=mesh['seq_0'=4,'seq_1'=16,'head'=8] {'seq_0'}, dimensions={0}, use_global_device_ids=true | all-gather | bytes 655360 | tf_op jit(solution)/shard_map/all_gather | solution.py:22
  102.9 0.6 fusion.15
  103.4 0.3 multiply_reduce_fusion.1
  103.8 10.4 %psum.14 = f32[256,1]{0,1:T(1,128)S(1)} all-reduce(f32[256,1]{0,1:T(1,128)S(1)} %bitcast.395), channel_id=1, replica_groups=mesh['seq_0'=4,'seq_1'=16,'head'=8] {'head'}, use_global_device_ids=true, to_apply=%region_1.2 | all-reduce | flops 256 | bytes 2048 | tf_op jit(solution)/shard_map/psum | solution.py:92
  114.2 0.6 multiply_multiply_fusion
  114.8 0.8 multiply_convert_fusion.1
  115.6 47.1 %all-gather.8.cloned.1.call-done = bf16[64,512,48]{1,2,0:T(8,128)(2,1)} async-done(((bf16[4,512,48]{1,2,0:T(8,128)(2,1)}), bf16[64,512,48]{1,2,0:T(8,128)(2,1)}) %all-gather.8.cloned.1.call-update) | async-done | bytes 3145744 | tf_op jit(solution)/shard_map/all_gather | solution.py:41
  162.7 2.2 copy.123
  164.9 1.0 convolution_convert_fusion.1
  166.0 0.2 copy.196
  166.2 25.0 %all_to_all.5 = bf16[8,256,384]{2,1,0:T(8,128)(2,1)S(1)} all-to-all(bf16[8,256,384]{2,1,0:T(8,128)(2,1)S(1)} %bitcast.376), channel_id=1, replica_groups=mesh['seq_0'=4,'seq_1'=16,'head'=8] {'head'}, dimensions={0} | all-to-all | bytes 3145728 | tf_op jit(solution)/shard_map/all_to_all | solution.py:59
  191.2 0.2 convert_reduce_fusion
  191.5 0.8 multiply_reduce_fusion.2
  192.3 0.0 all-gather.14.cloned.1.call-start
  192.3 2.1 copy.125
  194.4 10.5 %psum.15 = f32[256,1]{0,1:T(1,128)S(1)} all-reduce(f32[256,1]{0,1:T(1,128)S(1)} %bitcast.394), channel_id=1, replica_groups=mesh['seq_0'=4,'seq_1'=16,'head'=8] {'head'}, use_global_device_ids=true, to_apply=%region_4.5 | all-reduce | flops 256 | bytes 2048 | tf_op jit(solution)/shard_map/psum | solution.py:105
  204.9 14.0 %all-gather.10.cloned.1.call-done = bf16[256,3072]{1,0:T(8,128)(2,1)} async-done(((bf16[256,384]{1,0:T(8,128)(2,1)}), bf16[256,3072]{1,0:T(8,128)(2,1)}) %all-gather.10.cloned.1.call-update) | async-done | bytes 1572880 | tf_op jit(solution)/shard_map/all_gather | solution.py:100
  218.9 3.9 %multiply_reduce_fusion = (f32[512]{0:T(512)}, bf16[256,512]{1,0:T(8,128)(2,1)}) fusion(f32[256,512]{1,0:T(8,128)} %copy.125, f32[256]{0:T(256)S(1)} %bitcast.392, f32[256]{0:T(256)S(1)} %bitcast.397, f32[256]{0:T(256)} %bitcast.396, f32[512]{0:T(512)S(1)} %get-tuple-element.43, bf16[256,3072]{1,0:T(8,128)(2,1)} %all-gather.10.cloned.1.call-done, ...), kind=kOutput, calls=%fused_computation.26 | convolution fusion | flops 806616576 | bytes 5512192 | tf_op jit(solution)/shard_map/dot_general | solution.py:101
  222.8 1.1 copy.145
  223.9 0.2 fusion.9
  224.1 0.8 copy.133
  225.0 1.3 fusion.2
  226.3 0.3 convolution_bitcast_fusion.3
  226.6 0.2 fusion.8
  226.9 0.8 copy.140
  227.7 4.2 %fusion = bf16[1,512,3072]{2,1,0:T(8,128)(2,1)} fusion(bf16[256,3072]{1,0:T(8,128)(2,1)} %all-gather.10.cloned.1.call-done, f32[256,512]{1,0:T(8,128)S(1)} %copy-done.4, f32[512]{0:T(512)S(1)} %get-tuple-element.43, f32[256]{0:T(256)S(1)} %bitcast.393), kind=kOutput, calls=%fused_computation.1 | convolution fusion | flops 807272448 | bytes 5245952 | tf_op jit(solution)/shard_map/dot_general | solution.py:109
  231.9 0.2 fusion.95
  232.2 0.3 convolution_bitcast_fusion
  232.5 66.9 %all-gather.14.cloned.1.call-done = bf16[64,128,128]{2,1,0:T(8,128)(2,1)} async-done(((bf16[4,128,128]{2,1,0:T(8,128)(2,1)}), bf16[64,128,128]{2,1,0:T(8,128)(2,1)}) %all-gather.14.cloned.1.call-update) | async-done | bytes 2097168 | tf_op jit(solution)/shard_map/all_gather | solution.py:22
  299.3 2.1 fusion.71
  301.4 13.2 %all_gather.37 = bf16[4,4,128,128]{3,2,1,0:T(8,128)(2,1)S(1)} all-gather(bf16[1,4,128,128]{3,2,1,0:T(8,128)(2,1)S(1)} %fusion.71), channel_id=1, replica_groups=mesh['seq_0'=4,'seq_1'=16,'head'=8] {'seq_0'}, dimensions={0}, use_global_device_ids=true | all-gather | bytes 655360 | tf_op jit(solution)/shard_map/all_gather | solution.py:22
  314.6 0.6 fusion.21
  315.2 0.3 fusion.6
  315.5 0.8 copy.142
  316.3 0.2 fusion.7
  316.6 0.8 copy.141
  (40 shorter events, 0.2 us)
Async XLA Ops:
  7.2 16.8 %copy-start = (bf16[256,512]{1,0:T(8,128)(2,1)S(1)}, bf16[256,512]{1,0:T(8,128)(2,1)}, u32[]{:S(2)}) copy-start(bf16[256,512]{1,0:T(8,128)(2,1)} %param.6) | copy-start | bytes 786436
  7.2 16.8 %copy-start.12 = (bf16[256,512]{1,0:T(8,128)(2,1)S(1)}, bf16[256,512]{1,0:T(8,128)(2,1)}, u32[]{:S(2)}) copy-start(bf16[256,512]{1,0:T(8,128)(2,1)} %param.7) | copy-start | bytes 786436
  7.2 18.2 %copy-start.7 = (bf16[256,512]{1,0:T(8,128)(2,1)S(1)}, bf16[256,512]{1,0:T(8,128)(2,1)}, u32[]{:S(2)}) copy-start(bf16[256,512]{1,0:T(8,128)(2,1)} %param.8) | copy-start | bytes 786436
  7.2 16.7 %copy-start.16 = (bf16[512]{0:T(512)(128)(2,1)S(1)}, bf16[512]{0:T(512)(128)(2,1)}, u32[]{:S(2)}) copy-start(bf16[512]{0:T(512)(128)(2,1)} %param.9) | copy-start | bytes 3076
  7.2 80.5 %all-gather.12.cloned.1.call-start = ((), (), s32[]{:S(2)}) async-start(), calls=%async_computation.3 | async-start | bytes 2228224 | tf_op jit(solution)/shard_map/all_gather | solution.py:22
  8.4 17.3 %copy-start.5 = (bf16[256,512]{0,1:T(8,128)(2,1)}, bf16[256,512]{0,1:T(8,128)(2,1)S(1)}, u32[]{:S(2)}) copy-start(bf16[256,512]{0,1:T(8,128)(2,1)S(1)} %copy.193) | copy-start | bytes 786436
  10.4 152.4 %all-gather.8.cloned.1.call-start = ((), (), s32[]{:S(2)}) async-start(), calls=%async_computation.1 | async-start | bytes 3342336 | tf_op jit(solution)/shard_map/all_gather | solution.py:41
  23.8 195.1 %all-gather.10.cloned.1.call-start = ((), (), s32[]{:S(2)}) async-start(), calls=%async_computation.2 | async-start | bytes 1769472 | tf_op jit(solution)/shard_map/all_gather | solution.py:100
  24.0 0.6 copy-start.15
  24.6 0.8 copy-start.9
  87.7 15.2 %copy-start.2 = (bf16[64,128,128]{2,1,0:T(8,128)(2,1)S(1)}, bf16[64,128,128]{2,1,0:T(8,128)(2,1)}, u32[]{:S(2)}) copy-start(bf16[64,128,128]{2,1,0:T(8,128)(2,1)} %all-gather.12.cloned.1.call-done) | copy-start | bytes 6291460
  103.7 59.0 %copy-start.3 = (f32[256,4,128]{0,2,1:T(8,128)}, f32[256,4,128]{0,2,1:T(8,128)S(1)}, u32[]{:S(2)}) copy-start(f32[256,4,128]{0,2,1:T(8,128)S(1)} %get-tuple-element.46) | copy-start | bytes 1572868
  162.7 2.2 copy-start.11
  166.2 25.3 %copy-start.14 = (bf16[256,384]{1,0:T(8,128)(2,1)S(1)}, bf16[256,384]{1,0:T(8,128)(2,1)}, u32[]{:S(2)}) copy-start(bf16[256,384]{1,0:T(8,128)(2,1)} %param.11) | copy-start | bytes 589828
  192.3 107.1 %all-gather.14.cloned.1.call-start = ((), (), s32[]{:S(2)}) async-start(), calls=%async_computation.4 | async-start | bytes 2228224 | tf_op jit(solution)/shard_map/all_gather | solution.py:22
  222.8 3.6 %copy-start.6 = (bf16[256,512]{0,1:T(8,128)(2,1)S(1)}, bf16[256,512]{0,1:T(8,128)(2,1)}, u32[]{:S(2)}) copy-start(bf16[256,512]{0,1:T(8,128)(2,1)} %copy-done.5) | copy-start | bytes 786436
  225.0 2.8 copy-start.4
  227.7 4.2 %copy-start.10 = (bf16[4,256,256]{2,1,0:T(8,128)(2,1)S(1)}, bf16[4,256,256]{2,1,0:T(8,128)(2,1)}, u32[]{:S(2)}) copy-start(bf16[4,256,256]{2,1,0:T(8,128)(2,1)} %copy-done.9) | copy-start | bytes 1572868
  299.3 15.3 %copy-start.1 = (bf16[64,128,128]{2,1,0:T(8,128)(2,1)S(1)}, bf16[64,128,128]{2,1,0:T(8,128)(2,1)}, u32[]{:S(2)}) copy-start(bf16[64,128,128]{2,1,0:T(8,128)(2,1)} %all-gather.14.cloned.1.call-done) | copy-start | bytes 6291460
  301.4 13.8 %copy-start.13 = (bf16[256,512]{1,0:T(8,128)(2,1)S(1)}, bf16[256,512]{1,0:T(8,128)(2,1)}, u32[]{:S(2)}) copy-start(bf16[256,512]{1,0:T(8,128)(2,1)} %param.7) | copy-start | bytes 786436
  314.6 1.7 copy-start.8
Sparse Core Ops, SparseCore 0:
  10.7 76.9 all-gather.11
  90.4 72.3 all-gather.7
  192.4 26.4 all-gather.9
  225.0 74.2 all-gather.13
where the time goes:
time: 324 us
  waiting for transfers between devices  190 us (59%)
  blocking collectives  84.9 us (26%)
  matrix products  15.1 us (5%)
  between operations  14.1 us (4%)
  local copies, waits for them, and re-layouts  11.9 us (4%)
  other arithmetic  7.74 us (2%)
    all_gather x2, waiting for transfers between devices, carried_in(): pieces = lax.all_gather(total.astype(jnp.bfloat16), axis)  129 us
    all_gather x1, waiting for transfers between devices, gather_in_order(): pieces = lax.all_gather(pieces, axes[k], axis=0, tiled=True)  47.1 us
    all_gather x2, blocking collectives, carried_in(): pieces = lax.all_gather(total.astype(jnp.bfloat16), axis)  26.3 us
    all_to_all x1, blocking collectives, summed_on_arrival(): lax.all_to_all(in_blocks(shard, dim, length), axis, 0, 0, tiled=True)  25 us
    all_gather x1, waiting for transfers between devices, per_device(): out_grad = lax.all_gather(grad_local, 'head', axis=1, tiled=True)  14 us
    all_gather x1, blocking collectives, gather_in_order(): pieces = lax.all_gather(pieces, axes[k], axis=0, tiled=True)  12.7 us
    psum x1, blocking collectives, per_device(): inner = lax.psum(product, 'head') / inverse  10.5 us
    psum x1, blocking collectives, per_device(): squares = lax.psum(jnp.sum(mixed * mixed, axis=1, keepdims=True), 'head')  10.4 us
  transfers between devices with their start and end apart: 4, of which 4 were waited for; matrix products, arithmetic and copies ran while one was open for 5% of the time, Pallas kernels for 0%

commit v1 on v0

--- a/solution.py
+++ b/solution.py
@@ -38,7 +38,9 @@
 def gather_in_order(shard, axes, turns):
     pieces = shard[None]
     for k in turns:
-        pieces = lax.all_gather(pieces, axes[k], axis=0, tiled=True)
+        pieces = jnp.concatenate(
+            lax.all_to_all(jnp.stack([pieces] * lax.axis_size(axes[k])), axes[k], 0, 0), axis=0
+        )
     held = [lax.axis_size(axes[k]) for k in reversed(turns)]
     pieces = pieces.reshape(*held, *shard.shape)
     turned = sorted(range(len(turns)), key=lambda place: turns[len(turns) - 1 - place])

time: 324 us -> 387 us (1.19)
  waiting for transfers between devices: 190 us -> 232 us
  starting transfers between devices: 0.16 us -> 15.5 us
    all_gather x2, waiting for transfers between devices: 129 us -> 216 us  [carried_in(): pieces = lax.all_gather(total.astype(jnp.bfloat16), axis)]
    all_gather x1 -> x0, waiting for transfers between devices: 47.1 us -> none  [gather_in_order(): pieces = lax.all_gather(pieces, axes[k], axis=0, tiled=True)]
    all_to_all x0 -> x1, starting transfers between devices: none -> 15.3 us  [gather_in_order(): lax.all_to_all(jnp.stack([pieces] * lax.axis_size(axes[k])), axes[k], 0, 0)]
    all_gather x1 -> x0, blocking collectives: 12.7 us -> none  [gather_in_order(): pieces = lax.all_gather(pieces, axes[k], axis=0, tiled=True)]
    all_to_all x0 -> x1, blocking collectives: none -> 10.4 us  [gather_in_order(): lax.all_to_all(jnp.stack([pieces] * lax.axis_size(axes[k])), axes[k], 0, 0)]
  transfers between devices with their start and end apart: 4 -> 4, of which waited for: 4 -> 3; matrix products, arithmetic and copies ran while one was open for 5% -> 6% of each run, Pallas kernels for 0% -> 0%
where the time goes in v1:
time: 387 us; the launch traced here: 386 us
  waiting for transfers between devices  232 us (60%)
  blocking collectives  83.7 us (22%)
  matrix products  18.5 us (5%)
  starting transfers between devices  15.5 us (4%)
  between operations  14.1 us (4%)
  local copies, waits for them, and re-layouts  13.7 us (4%)
  other arithmetic  8.77 us (2%)
    all_gather x2, waiting for transfers between devices, carried_in(): pieces = lax.all_gather(total.astype(jnp.bfloat16), axis)  216 us
    all_gather x2, blocking collectives, carried_in(): pieces = lax.all_gather(total.astype(jnp.bfloat16), axis)  26.8 us
    all_to_all x1, blocking collectives, summed_on_arrival(): lax.all_to_all(in_blocks(shard, dim, length), axis, 0, 0, tiled=True)  26 us
    all_gather x1, waiting for transfers between devices, per_device(): out_grad = lax.all_gather(grad_local, 'head', axis=1, tiled=True)  15.4 us
    all_to_all x1, starting transfers between devices, gather_in_order(): lax.all_to_all(jnp.stack([pieces] * lax.axis_size(axes[k])), axes[k], 0, 0)  15.3 us
    psum x1, blocking collectives, per_device(): inner = lax.psum(product, 'head') / inverse  10.5 us
    all_to_all x1, blocking collectives, gather_in_order(): lax.all_to_all(jnp.stack([pieces] * lax.axis_size(axes[k])), axes[k], 0, 0)  10.4 us
    psum x1, blocking collectives, per_device(): squares = lax.psum(jnp.sum(mixed * mixed, axis=1, keepdims=True), 'head')  9.99 us
  transfers between devices with their start and end apart: 4, of which 3 were waited for; matrix products, arithmetic and copies ran while one was open for 6% of the time, Pallas kernels for 0%

profile of v1, /device:TPU:8, one launch (start us, length us, event | category | flops | bytes accessed | tf_op | source)
XLA Modules:
  0.0 386.0 jit_solution(49492116282056873)
XLA Ops:
  7.2 0.9 stack.6
  8.0 10.4 %all_to_all.15 = bf16[4,1,512,48]{2,3,1,0:T(8,128)(2,1)S(1)} all-to-all(bf16[4,1,512,48]{2,3,1,0:T(8,128)(2,1)S(1)} %stack.6), channel_id=1, replica_groups=mesh['seq_0'=4,'seq_1'=16,'head'=8] {'seq_0'}, dimensions={0} | all-to-all | bytes 393216 | tf_op jit(solution)/shard_map/all_to_all | solution.py:42
  18.5 2.0 stack.7
  20.5 15.3 %all-to-all-start.1 = ((bf16[16,4,512,48]{2,3,1,0:T(8,128)(2,1)}), bf16[16,4,512,48]{2,3,1,0:T(8,128)(2,1)S(1)}, u32[]{:S(2)}, u32[]{:S(2)}) async-start(bf16[16,4,512,48]{2,3,1,0:T(8,128)(2,1)} %stack.7), calls=%async_computation.1 | async-start | bytes 6291456 | tf_op jit(solution)/shard_map/all_to_all | solution.py:42
  35.8 0.0 all-gather.8.cloned.1.call-start
  35.9 1.8 copy.138
  37.7 1.9 convolution_convert_fusion.3
  39.8 0.6 copy-done.14
  40.4 1.2 fusion.1
  41.6 0.8 copy-done.8
  42.4 2.1 convolution_bitcast_fusion.5
  44.5 149.5 %all-gather.8.cloned.1.call-done = bf16[64,128,128]{2,1,0:T(8,128)(2,1)} async-done(((bf16[4,128,128]{2,1,0:T(8,128)(2,1)}), bf16[64,128,128]{2,1,0:T(8,128)(2,1)}) %all-gather.8.cloned.1.call-update) | async-done | bytes 2097168 | tf_op jit(solution)/shard_map/all_gather | solution.py:22
  193.9 2.1 fusion.46
  196.0 13.6 %all_gather.25 = bf16[4,4,128,128]{3,2,1,0:T(8,128)(2,1)S(1)} all-gather(bf16[1,4,128,128]{3,2,1,0:T(8,128)(2,1)S(1)} %fusion.46), channel_id=1, replica_groups=mesh['seq_0'=4,'seq_1'=16,'head'=8] {'seq_0'}, dimensions={0}, use_global_device_ids=true | all-gather | bytes 655360 | tf_op jit(solution)/shard_map/all_gather | solution.py:22
  209.6 0.6 fusion.15
  210.2 1.1 multiply_reduce_fusion.1
  211.3 10.0 %psum.14 = f32[256,1]{0,1:T(1,128)S(1)} all-reduce(f32[256,1]{0,1:T(1,128)S(1)} %bitcast.389), channel_id=1, replica_groups=mesh['seq_0'=4,'seq_1'=16,'head'=8] {'head'}, use_global_device_ids=true, to_apply=%region_1.2 | all-reduce | flops 256 | bytes 2048 | tf_op jit(solution)/shard_map/psum | solution.py:94
  221.2 0.6 multiply_multiply_fusion
  221.8 1.9 multiply_convert_fusion.1
  223.7 0.3 copy.70
  224.0 0.7 copy-done.11
  224.7 1.0 convolution_convert_fusion.1
  225.7 0.2 copy.141
  225.9 26.0 %all_to_all.16 = bf16[8,256,384]{2,1,0:T(8,128)(2,1)S(1)} all-to-all(bf16[8,256,384]{2,1,0:T(8,128)(2,1)S(1)} %bitcast.372), channel_id=1, replica_groups=mesh['seq_0'=4,'seq_1'=16,'head'=8] {'head'}, dimensions={0} | all-to-all | bytes 3145728 | tf_op jit(solution)/shard_map/all_to_all | solution.py:61
  251.9 0.2 convert_reduce_fusion
  252.1 0.8 multiply_reduce_fusion.2
  253.0 2.0 copy.72
  255.0 10.5 %psum.15 = f32[256,1]{0,1:T(1,128)S(1)} all-reduce(f32[256,1]{0,1:T(1,128)S(1)} %bitcast.388), channel_id=1, replica_groups=mesh['seq_0'=4,'seq_1'=16,'head'=8] {'head'}, use_global_device_ids=true, to_apply=%region_4.5 | all-reduce | flops 256 | bytes 2048 | tf_op jit(solution)/shard_map/psum | solution.py:107
  265.5 15.4 %all-gather.6.cloned.1.call-done = bf16[256,3072]{1,0:T(8,128)(2,1)} async-done(((bf16[256,384]{1,0:T(8,128)(2,1)}), bf16[256,3072]{1,0:T(8,128)(2,1)}) %all-gather.6.cloned.1.call-update) | async-done | bytes 1572880 | tf_op jit(solution)/shard_map/all_gather | solution.py:102
  280.9 3.9 %multiply_reduce_fusion = (f32[512]{0:T(512)}, bf16[256,512]{1,0:T(8,128)(2,1)}) fusion(f32[256,512]{1,0:T(8,128)} %copy.72, f32[256]{0:T(256)S(1)} %bitcast.386, f32[256]{0:T(256)S(1)} %bitcast.391, f32[256]{0:T(256)} %bitcast.390, f32[512]{0:T(512)S(1)} %get-tuple-element.31, bf16[256,3072]{1,0:T(8,128)(2,1)} %all-gather.6.cloned.1.call-done, ...), kind=kOutput, calls=%fused_computation.26 | convolution fusion | flops 806616576 | bytes 5512192 | tf_op jit(solution)/shard_map/dot_general | solution.py:103
  284.8 1.1 copy.92
  286.0 0.2 fusion.9
  286.2 0.8 copy.80
  287.0 1.3 fusion.2
  288.4 0.3 convolution_bitcast_fusion.3
  288.7 0.2 fusion.8
  288.9 0.8 copy.87
  289.8 4.2 %fusion = bf16[1,512,3072]{2,1,0:T(8,128)(2,1)} fusion(bf16[256,3072]{1,0:T(8,128)(2,1)} %all-gather.6.cloned.1.call-done, f32[256,512]{1,0:T(8,128)S(1)} %copy-done.5, f32[512]{0:T(512)S(1)} %get-tuple-element.31, f32[256]{0:T(256)S(1)} %bitcast.387), kind=kOutput, calls=%fused_computation.1 | convolution fusion | flops 807272448 | bytes 5245952 | tf_op jit(solution)/shard_map/dot_general | solution.py:111
  294.0 0.3 convolution_bitcast_fusion
  294.3 0.2 fusion.95
  294.5 66.9 %all-gather.10.cloned.1.call-done = bf16[64,128,128]{2,1,0:T(8,128)(2,1)} async-done(((bf16[4,128,128]{2,1,0:T(8,128)(2,1)}), bf16[64,128,128]{2,1,0:T(8,128)(2,1)}) %all-gather.10.cloned.1.call-update) | async-done | bytes 2097168 | tf_op jit(solution)/shard_map/all_gather | solution.py:22
  361.4 2.1 fusion.71
  363.5 13.2 %all_gather.29 = bf16[4,4,128,128]{3,2,1,0:T(8,128)(2,1)S(1)} all-gather(bf16[1,4,128,128]{3,2,1,0:T(8,128)(2,1)S(1)} %fusion.71), channel_id=1, replica_groups=mesh['seq_0'=4,'seq_1'=16,'head'=8] {'seq_0'}, dimensions={0}, use_global_device_ids=true | all-gather | bytes 655360 | tf_op jit(solution)/shard_map/all_gather | solution.py:22
  376.7 0.6 fusion.21
  377.3 0.2 fusion.7
  377.5 0.8 copy.88
  378.4 0.3 fusion.6
  378.6 0.8 copy.89
  (38 shorter events, 0.2 us)
Async XLA Ops:
  7.2 33.2 %copy-start = (bf16[256,512]{1,0:T(8,128)(2,1)S(1)}, bf16[256,512]{1,0:T(8,128)(2,1)}, u32[]{:S(2)}) copy-start(bf16[256,512]{1,0:T(8,128)(2,1)} %param.6) | copy-start | bytes 786436
  20.5 19.2 %copy-start.15 = (bf16[512]{0:T(512)(128)(2,1)S(1)}, bf16[512]{0:T(512)(128)(2,1)}, u32[]{:S(2)}) copy-start(bf16[512]{0:T(512)(128)(2,1)} %param.9) | copy-start | bytes 3076
  20.5 203.2 %all-to-all-start.1 = ((bf16[16,4,512,48]{2,3,1,0:T(8,128)(2,1)}), bf16[16,4,512,48]{2,3,1,0:T(8,128)(2,1)S(1)}, u32[]{:S(2)}, u32[]{:S(2)}) async-start(bf16[16,4,512,48]{2,3,1,0:T(8,128)(2,1)} %stack.7), calls=%async_computation.1 | async-start | bytes 6291456 | tf_op jit(solution)/shard_map/all_to_all | solution.py:42
  35.8 158.1 %all-gather.8.cloned.1.call-start = ((), (), s32[]{:S(2)}) async-start(), calls=%async_computation.4 | async-start | bytes 2228224 | tf_op jit(solution)/shard_map/all_gather | solution.py:22
  39.6 241.3 %all-gather.6.cloned.1.call-start = ((), (), s32[]{:S(2)}) async-start(), calls=%async_computation.3 | async-start | bytes 1769472 | tf_op jit(solution)/shard_map/all_gather | solution.py:102
  39.7 0.6 copy-start.14
  41.6 0.8 copy-start.8
  193.9 15.7 %copy-start.4 = (bf16[64,128,128]{2,1,0:T(8,128)(2,1)S(1)}, bf16[64,128,128]{2,1,0:T(8,128)(2,1)}, u32[]{:S(2)}) copy-start(bf16[64,128,128]{2,1,0:T(8,128)(2,1)} %all-gather.8.cloned.1.call-done) | copy-start | bytes 6291460
  196.0 14.2 %copy-start.10 = (f32[256,4,128]{0,2,1:T(8,128)S(1)}, f32[256,4,128]{0,2,1:T(8,128)}, u32[]{:S(2)}) copy-start(f32[256,4,128]{0,2,1:T(8,128)} %convolution_bitcast_fusion.5) | copy-start | bytes 1572868
  223.7 1.0 copy-start.11
  224.0 1.7 copy-start.1
  225.9 26.2 %copy-start.13 = (bf16[256,384]{1,0:T(8,128)(2,1)S(1)}, bf16[256,384]{1,0:T(8,128)(2,1)}, u32[]{:S(2)}) copy-start(bf16[256,384]{1,0:T(8,128)(2,1)} %param.11) | copy-start | bytes 589828
  251.9 29.0 %copy-start.2 = (bf16[16,4,512,48]{2,3,0,1:T(8,128)(2,1)S(1)}, bf16[16,4,512,48]{2,3,0,1:T(8,128)(2,1)}, u32[]{:S(2)}) copy-start(bf16[16,4,512,48]{2,3,0,1:T(8,128)(2,1)} %copy-done.1) | copy-start | bytes 9437188
  252.9 108.5 %all-gather.10.cloned.1.call-start = ((), (), s32[]{:S(2)}) async-start(), calls=%async_computation.5 | async-start | bytes 2228224 | tf_op jit(solution)/shard_map/all_gather | solution.py:22
  284.8 3.6 copy-start.6
  287.0 2.8 copy-start.5
  289.8 4.5 %copy-start.9 = (bf16[4,256,256]{2,1,0:T(8,128)(2,1)S(1)}, bf16[4,256,256]{2,1,0:T(8,128)(2,1)}, u32[]{:S(2)}) copy-start(bf16[4,256,256]{2,1,0:T(8,128)(2,1)} %copy-done.8) | copy-start | bytes 1572868
  361.4 15.3 %copy-start.3 = (bf16[64,128,128]{2,1,0:T(8,128)(2,1)S(1)}, bf16[64,128,128]{2,1,0:T(8,128)(2,1)}, u32[]{:S(2)}) copy-start(bf16[64,128,128]{2,1,0:T(8,128)(2,1)} %all-gather.10.cloned.1.call-done) | copy-start | bytes 6291460
  363.5 13.8 %copy-start.7 = (bf16[256,512]{1,0:T(8,128)(2,1)S(1)}, bf16[256,512]{1,0:T(8,128)(2,1)}, u32[]{:S(2)}) copy-start(bf16[256,512]{1,0:T(8,128)(2,1)} %param.8) | copy-start | bytes 786436
  376.7 1.7 copy-start.12
Sparse Core Ops, SparseCore 0:
  39.7 154.1 all-gather.7
  253.1 27.8 all-gather.5
  287.1 74.2 all-gather.9
